TPU v7x, 32 devices: a whole 2x2x4 slice. The times are simulated.
32 devices in a mesh: path: 8 (over y, x, core), mod: 4 (over z).
Axes of the slice: x: 2, y: 2, z: 4, core: 2. Of those that a mesh axis runs over, the one named last changes fastest.
Arguments:
- activations: bfloat16 [8, 512, 4096], P('path', 'mod'), may hold values from -6 to 6
- cotangent: bfloat16 [8, 512, 4096], P('path', 'mod'), may hold values from -6 to 6
- first_weight: bfloat16 [8, 4096, 4096], P('path', None, 'mod'), may hold values from -6 to 6
- second_weight: bfloat16 [8, 4096, 4096], P('path', None, 'mod'), may hold values from -6 to 6
- first_master: float32 [4, 4096, 4096], P(None, ('path', 'mod')), may hold values from -6 to 6
- second_master: float32 [4, 4096, 4096], P(None, ('path', 'mod')), may hold values from -6 to 6
- first_moment: float32 [4, 4096, 4096], P(None, ('path', 'mod')), may hold values from -3 to 3
- second_moment: float32 [4, 4096, 4096], P(None, ('path', 'mod')), may hold values from -3 to 3
- routing: int32 [8, 2], replicated, may hold values from 0 to 3, as said below
Outputs:
- first_result: bfloat16 [8, 4096, 4096], P('path', None, 'mod')
- second_result: bfloat16 [8, 4096, 4096], P('path', None, 'mod')
Inputs may be any that keep to these rules, and one draw needn't show every extreme that they name: `routing`: for each of the two levels, every one of the 4 modules is taken by at least one path.
All inputs are finite; a program needn't handle non-finite values.
Results may differ from a plain program's by a relative error of at most 0.0045.
Values may be sent and summed in bfloat16 or wider, within the bound.
A program may use at most 192 MiB of HBM per device.

v0:
```python
import jax
import jax.numpy as jnp
from jax import lax
from jax.sharding import PartitionSpec as P

inner_rate = 1.0
outer_rate = 0.7
momentum_decay = 0.9


def to_owners(stacked, onehot):
    level_count = stacked.shape[0]
    columns = stacked.shape[2]
    path_count = onehot.shape[1]
    groups = lax.axis_size("mod")
    arrived = lax.all_to_all(stacked, ("path", "mod"), split_axis=1, concat_axis=2, tiled=True)
    owned_rows = arrived.shape[1]
    arrived = arrived.reshape(level_count, owned_rows, path_count, groups, columns)
    summed = jnp.einsum("lrpkc,lpm->lmrkc", arrived, onehot, preferred_element_type=jnp.float32)
    return summed.reshape(level_count, onehot.shape[2], owned_rows, groups * columns)


def outer_step(summed, onehot, master, moment):
    path_total = jnp.sum(onehot.astype(jnp.float32), axis=1)[:, :, None, None]
    outer = master - summed / path_total
    moment_new = momentum_decay * moment + outer
    return (master - outer_rate * (outer + momentum_decay * moment_new)).astype(jnp.bfloat16)


def to_paths(renewed, onehot):
    level_count, module_count, owned_rows, model_width = renewed.shape
    groups = lax.axis_size("mod")
    path_count = onehot.shape[1]
    columns = model_width // groups
    split = renewed.reshape(level_count, module_count, owned_rows, groups, columns)
    chosen = jnp.einsum(
        "lmrkc,lpm->lrpkc", split, onehot, preferred_element_type=jnp.float32
    ).astype(jnp.bfloat16)
    outgoing = chosen.reshape(level_count, owned_rows, path_count * groups * columns)
    return lax.all_to_all(outgoing, ("path", "mod"), split_axis=2, concat_axis=1, tiled=True)


def body(
    activations,
    cotangent,
    first_weight,
    second_weight,
    first_master,
    second_master,
    first_moment,
    second_moment,
    routing,
):
    inputs_full, upstream = (
        lax.all_gather(activations, "mod", axis=1, tiled=True),
        lax.all_gather(cotangent, "mod", axis=1, tiled=True),
    )
    inputs_full = inputs_full[0]
    upstream = upstream[0]
    weight_in = first_weight[0]
    weight_out = second_weight[0]
    scale = inputs_full.shape[1] ** (-0.5)
    pre = jnp.dot(inputs_full, weight_in, preferred_element_type=jnp.float32) * scale
    hidden = jax.nn.silu(pre).astype(jnp.bfloat16)
    grad_hidden = jnp.dot(upstream, weight_out, preferred_element_type=jnp.float32) * scale
    grad_out = (
        lax.dot_general(
            upstream, hidden, (((0,), (0,)), ((), ())), preferred_element_type=jnp.float32
        )
        * scale
    )
    trained_out = (weight_out.astype(jnp.float32) - inner_rate * grad_out).astype(jnp.bfloat16)
    sigma = jax.nn.sigmoid(pre)
    grad_pre = (grad_hidden * sigma * (1.0 + pre * (1.0 - sigma))).astype(jnp.bfloat16)
    grad_in = (
        lax.dot_general(
            inputs_full, grad_pre, (((0,), (0,)), ((), ())), preferred_element_type=jnp.float32
        )
        * scale
    )
    trained_in = (weight_in.astype(jnp.float32) - inner_rate * grad_in).astype(jnp.bfloat16)
    module_count = first_master.shape[0]
    module_ids = jnp.arange(module_count)
    onehot = (jnp.transpose(routing)[:, :, None] == module_ids[None, None, :]).astype(jnp.bfloat16)
    summed = to_owners(jnp.stack((trained_in, trained_out)), onehot)
    renewed = outer_step(
        summed,
        onehot,
        jnp.stack((first_master, second_master)),
        jnp.stack((first_moment, second_moment)),
    )
    returned = to_paths(renewed, onehot)
    first_back = returned[0]
    second_back = returned[1]
    return (first_back[None], second_back[None])


def solution(mesh):
    return jax.shard_map(
        body,
        mesh=mesh,
        in_specs=(
            P("path", "mod", None),
            P("path", "mod", None),
            P("path", None, "mod"),
            P("path", None, "mod"),
            P(None, ("path", "mod"), None),
            P(None, ("path", "mod"), None),
            P(None, ("path", "mod"), None),
            P(None, ("path", "mod"), None),
            P(),
        ),
        out_specs=(P("path", None, "mod"), P("path", None, "mod")),
        check_vma=False,
    )
```

profile of v0, /device:TPU:1, one launch (start us, length us, event | category | flops | bytes accessed | tf_op | source)
XLA Modules:
  0.0 1153.4 jit_solution(4697887328991194632)
XLA Ops:
  7.2 0.7 all-gather.5.cloned.1.call-update
  7.9 0.0 all-gather.3.cloned.1.call-start
  7.9 0.7 all-gather.3.cloned.1.call-update
  8.6 12.0 %copy.45 = bf16[1,4096,1024]{1,2,0:T(8,128)(2,1)} copy(bf16[1,4096,1024]{2,1,0:T(8,128)(2,1)} %param.11) | data formatting | bytes 16777216 | tf_op args[2]
  20.6 11.9 %copy.46 = bf16[1,4096,1024]{1,2,0:T(8,128)(2,1)} copy(bf16[1,4096,1024]{2,1,0:T(8,128)(2,1)} %param.12) | data formatting | bytes 16777216 | tf_op args[3]
  32.6 59.7 %all-gather.5.cloned.1.call-done = bf16[1,512,4096]{2,1,0:T(8,128)(2,1)} async-done(((bf16[1,128,4096]{2,1,0:T(8,128)(2,1)}), bf16[1,512,4096]{2,1,0:T(8,128)(2,1)}) %all-gather.5.cloned.1.call-update) | async-done | bytes 4194320 | tf_op jit(solution)/shard_map/all_gather | solution.py:55
  92.2 8.1 fusion.14
  100.4 72.7 %all-gather.3.cloned.1.call-done = bf16[1,512,4096]{2,1,0:T(8,128)(2,1)} async-done(((bf16[1,128,4096]{2,1,0:T(8,128)(2,1)}), bf16[1,512,4096]{2,1,0:T(8,128)(2,1)}) %all-gather.3.cloned.1.call-update) | async-done | bytes 4194320 | tf_op jit(solution)/shard_map/all_gather | solution.py:56
  173.1 18.0 %fusion.18 = bf16[1,4096,1024]{1,2,0:T(8,128)(2,1)} fusion(bf16[1,4096,1024]{1,2,0:T(8,128)(2,1)} %copy.45, bf16[1,512,4096]{2,1,0:T(8,128)(2,1)} %all-gather.5.cloned.1.call-done, f32[512,1024]{1,0:T(8,128)S(1)} %fusion.14, bf16[1,4096,1024]{2,1,0:T(8,128)(2,1)} %param.12, bf16[1,512,4096]{2,1,0:T(8,128)(2,1)} %all-gather.3.cloned.1.call-done), kind=kOutput, calls=%fused_computation.21 | convolution fusion | flops 8612478976 | bytes 35651584 | tf_op jit(solution)/shard_map/dot_general | solution.py:76
  191.1 11.1 fusion.19
  202.1 10.5 pad_maximum_fusion.1
  212.6 41.5 %copy.47 = bf16[2,4096,1024]{2,0,1:T(2,128)(2,1)} copy(bf16[2,4096,1024]{1,2,0:T(8,128)(2,1)} %pad_maximum_fusion.1) | data formatting | bytes 33554432 | tf_op jit(solution)/shard_map/stack | solution.py:85
  254.1 4.2 all-to-all-start
  258.4 8.9 copy.41
  267.3 10.4 copy.43
  277.7 8.9 copy.42
  286.6 10.3 copy.44
  296.9 8.9 copy.50
  305.8 10.4 copy.52
  316.2 8.9 copy.51
  325.0 10.3 copy.53
  335.3 0.1 convert_reduce_fusion
  335.4 280.1 %all-to-all-done = bf16[2,4096,1024]{2,0,1:T(2,128)(2,1)} async-done(((bf16[2,4096,1024]{2,0,1:T(2,128)(2,1)}), bf16[2,4096,1024]{2,0,1:T(2,128)(2,1)}, u32[]{:S(2)}, u32[]{:S(2)}) %all-to-all-start) | async-done | bytes 16777248 | tf_op jit(solution)/shard_map/all_to_all | solution.py:16
  615.5 16.4 %copy.48 = bf16[2,4096,1024]{2,1,0:T(8,128)(2,1)} copy(bf16[2,4096,1024]{2,0,1:T(2,128)(2,1)} %all-to-all-done) | data formatting | bytes 33554432 | tf_op jit(solution)/shard_map/all_to_all | solution.py:16
  632.0 40.2 %convert_bitcast_fusion = bf16[2,128,8,4,1024]{4,2,3,1,0:T(8,128)(2,1)} fusion(f32[1,4,128,4,1024]{4,1,3,2,0:T(4,128)} %copy.53, f32[1,4,128,4,1024]{4,1,3,2,0:T(4,128)} %copy.52, bf16[2,128,8,4,1024]{4,1,3,2,0:T(8,128)(2,1)} %bitcast.86, f32[1,4,128,4,1024]{4,1,3,2,0:T(4,128)} %copy.44, f32[1,4,128,4,1024]{4,1,3,2,0:T(4,128)} %copy.43, ...), kind=kOutput, calls=%fused_computation.15 | convolution fusion | flops 188743808 | bytes 67108960 | tf_op jit(solution)/shard_map/lmrkc,lpm->lrpkc/dot_general | solution.py:36
  672.2 23.0 %copy.54 = bf16[2,128,8,4,1024]{1,4,3,2,0:T(8,128)(2,1)} copy(bf16[2,128,8,4,1024]{4,2,3,1,0:T(8,128)(2,1)} %convert_bitcast_fusion) | data formatting | bytes 33554432 | tf_op jit(solution)/shard_map/convert_element_type | solution.py:38
  695.2 30.0 %copy.55 = bf16[2,128,32768]{1,0,2:T(2,128)(2,1)S(1)} copy(bf16[2,128,32768]{1,2,0:T(8,128)(2,1)} %bitcast.81) | data formatting | bytes 33554432 | tf_op jit(solution)/shard_map/reshape | solution.py:39
  725.2 381.5 %all_to_all.30 = bf16[2,128,32768]{1,0,2:T(2,128)(2,1)} all-to-all(bf16[2,128,32768]{1,0,2:T(2,128)(2,1)S(1)} %copy.55), channel_id=1, replica_groups=mesh['path'=8,'mod'=4] {'path','mod'}, dimensions={2} | all-to-all | bytes 33554432 | tf_op jit(solution)/shard_map/all_to_all | solution.py:40
  1106.8 9.6 copy.56
  1116.4 6.3 fusion.51
  1122.7 11.9 %copy.57 = bf16[1,32,128,1024]{3,2,1,0:T(8,128)(2,1)} copy(bf16[1,32,128,1024]{2,3,1,0:T(8,128)(2,1)} %get-tuple-element.3) | data formatting | bytes 16777216 | tf_op jit(solution)/shard_map/slice | solution.py:93
  1134.6 11.9 %copy.58 = bf16[1,32,128,1024]{3,2,1,0:T(8,128)(2,1)} copy(bf16[1,32,128,1024]{2,3,1,0:T(8,128)(2,1)} %get-tuple-element.2) | data formatting | bytes 16777216 | tf_op jit(solution)/shard_map/slice | solution.py:94
  (5 shorter events, 0.0 us)
Async XLA Ops:
  7.2 85.1 %all-gather.5.cloned.1.call-start = ((), (), s32[]{:S(2)}) async-start(), calls=%async_computation.3 | async-start | bytes 5242880 | tf_op jit(solution)/shard_map/all_gather | solution.py:55
  7.9 165.2 %all-gather.3.cloned.1.call-start = ((), (), s32[]{:S(2)}) async-start(), calls=%async_computation.2 | async-start | bytes 5242880 | tf_op jit(solution)/shard_map/all_gather | solution.py:56
  191.1 11.1 copy-start
  254.1 361.4 %all-to-all-start = ((bf16[2,4096,1024]{2,0,1:T(2,128)(2,1)}), bf16[2,4096,1024]{2,0,1:T(2,128)(2,1)}, u32[]{:S(2)}, u32[]{:S(2)}) async-start(bf16[2,4096,1024]{2,0,1:T(2,128)(2,1)} %copy.47), calls=%async_computation | async-start | bytes 33554432 | tf_op jit(solution)/shard_map/all_to_all | solution.py:16
  325.0 10.3 copy-start.1
Sparse Core Ops, SparseCore 0:
  9.5 82.6 all-gather.4
  93.8 79.2 all-gather.2
where the time goes:
time: 1160 us; the launch traced here: 1150 us
  waiting for transfers between devices  414 us (36%)
  blocking collectives  382 us (33%)
  local copies, waits for them, and re-layouts  252 us (22%)
  matrix products  77.4 us (7%)
  between operations  14.1 us (1%)
    all_to_all x1, blocking collectives, to_paths(): lax.all_to_all(outgoing, ('path', 'mod'), split_axis=2, concat_axis=1, ti...  382 us
    all_to_all x1, waiting for transfers between devices, to_owners(): lax.all_to_all(stacked, ('path', 'mod'), split_axis=1, concat_axis=2, til...  280 us
    all_gather x1, waiting for transfers between devices, body(): lax.all_gather(cotangent, 'mod', axis=1, tiled=True)  72.7 us
    all_gather x1, waiting for transfers between devices, body(): lax.all_gather(activations, 'mod', axis=1, tiled=True)  59.7 us
    unnamed x10, local copies, waits for them, and re-layouts  59.5 us
    another operation x1, local copies, waits for them, and re-layouts, body(): summed = to_owners(jnp.stack((trained_in, trained_out)), onehot)  41.5 us
    dot_general x1, matrix products, to_paths(): jnp.einsum('lmrkc,lpm->lrpkc', split, onehot, preferred_element_type=jnp....  40.2 us
    reshape x1, local copies, waits for them, and re-layouts, to_paths(): chosen.reshape(level_count, owned_rows, path_count * groups * columns)  30 us
  transfers between devices with their start and end apart: 3, of which 3 were waited for; matrix products, arithmetic and copies ran while one was open for 9% of the time, Pallas kernels for 0%

commit v1 on v0

v1 whole, which is shorter than its diff:
```python
import functools

import jax
import jax.numpy as jnp
from jax import lax
from jax.experimental import pallas as pl
from jax.experimental.pallas import tpu as pltpu
from jax.sharding import PartitionSpec as P

inner_rate = 1.0
outer_rate = 0.7
momentum_decay = 0.9

mean_factor = outer_rate * (1.0 + momentum_decay)
master_factor = 1.0 - mean_factor
moment_factor = -outer_rate * momentum_decay * momentum_decay

ANY = pl.BlockSpec(memory_space=pl.ANY)


def remote(src, dst, send_sem, recv_sem, where):
    return pltpu.make_async_remote_copy(
        src_ref=src,
        dst_ref=dst,
        send_sem=send_sem,
        recv_sem=recv_sem,
        device_id=where,
        device_id_type=pl.DeviceIdType.MESH,
    )


def run_all(copies):
    for copy in copies:
        copy.start()
    for copy in copies:
        copy.wait()


def scatter_kernel(
    paths, groups, t0, t1, b0, b1, a0, a1, c0, c1, send, recv, zsend, zrecv, local
):
    p = lax.axis_index("path")
    z = lax.axis_index("mod")
    rows = a0.shape[1]
    owned = b0.shape[1]
    columns = a0.shape[2]
    copies = []
    locals_ = []
    for level, (t, a) in enumerate(((t0, a0), (t1, a1))):
        own = t.at[pl.ds(p * rows, rows), :]
        locals_.append(pltpu.make_async_copy(own, a.at[p], local.at[level]))
    for level, (b, c) in enumerate(((b0, c0), (b1, c1))):
        own = b.at[:, :, pl.ds(pl.multiple_of(z * columns, columns), columns)]
        locals_.append(
            pltpu.make_async_copy(own, c.at[:, pl.ds(z * owned, owned), :], local.at[2 + level])
        )
    for level, (b, c) in enumerate(((b0, c0), (b1, c1))):
        for step in range(1, groups):
            to = lax.rem(z + step, groups)
            copies.append(
                remote(
                    b.at[:, :, pl.ds(pl.multiple_of(to * columns, columns), columns)],
                    c.at[:, pl.ds(z * owned, owned), :],
                    zsend.at[level, step],
                    zrecv.at[level, step],
                    (p, to),
                )
            )
    order = []
    for level, (t, a) in enumerate(((t0, a0), (t1, a1))):
        for step in range(paths - 1, 0, -1):
            to = lax.rem(p + step, paths)
            order.append(
                remote(
                    t.at[pl.ds(to * rows, rows), :],
                    a.at[p],
                    send.at[level, step],
                    recv.at[level, step],
                    (to, z),
                )
            )
    run_all(order + copies + locals_)


def scatter(t0, t1, b0, b1):
    paths = lax.axis_size("path")
    groups = lax.axis_size("mod")
    depth, columns = t0.shape
    modules = b0.shape[0]
    rows = depth // paths
    arrived = jax.ShapeDtypeStruct((paths, rows, columns), t0.dtype)
    base = jax.ShapeDtypeStruct((modules, rows, columns), b0.dtype)
    dma = pltpu.SemaphoreType.DMA
    return pl.pallas_call(
        functools.partial(scatter_kernel, paths, groups),
        out_shape=(arrived, arrived, base, base),
        in_specs=[ANY] * 4,
        out_specs=[ANY] * 4,
        scratch_shapes=[dma((2, paths)), dma((2, paths)), dma((2, groups)), dma((2, groups)), dma((4,))],
        compiler_params=pltpu.CompilerParams(has_side_effects=True),
        name="scatter",
    )(t0, t1, b0, b1)


def gather_kernel(paths, v0, v1, r0, r1, send, recv, local):
    p = lax.axis_index("path")
    z = lax.axis_index("mod")
    rows = v0.shape[1]
    copies = []
    locals_ = []
    for level, (v, r) in enumerate(((v0, r0), (v1, r1))):
        mine = r.at[pl.ds(p * rows, rows), :]
        locals_.append(pltpu.make_async_copy(v.at[p], mine, local.at[level]))
        for step in range(paths - 1, 0, -1):
            to = lax.rem(p + step, paths)
            copies.append(
                remote(v.at[to], mine, send.at[level, step], recv.at[level, step], (to, z))
            )
    run_all(copies + locals_)


def gather(v0, v1):
    paths, rows, columns = v0.shape
    result = jax.ShapeDtypeStruct((paths * rows, columns), v0.dtype)
    dma = pltpu.SemaphoreType.DMA
    return pl.pallas_call(
        functools.partial(gather_kernel, paths),
        out_shape=(result, result),
        in_specs=[ANY] * 2,
        out_specs=[ANY] * 2,
        scratch_shapes=[dma((2, paths)), dma((2, paths)), dma((2,))],
        compiler_params=pltpu.CompilerParams(has_side_effects=True),
        name="gather",
    )(v0, v1)


def combine_kernel(level, routing, factor, arrived, base, out, total, fresh):
    paths = arrived.shape[0]
    modules = base.shape[0]
    total[...] = jnp.zeros_like(total)
    for q in range(paths):
        m = routing[q, level]
        total[m] = total[m] + arrived[q].astype(jnp.float32)
    for m in range(modules):
        fresh[m] = (base[m].astype(jnp.float32) + factor[level, m] * total[m]).astype(out.dtype)
    for q in range(paths):
        out[q] = fresh[routing[q, level]]


def combine(level, routing, factor, arrived, base):
    paths, rows, columns = arrived.shape
    modules = base.shape[0]
    block = min(rows, 64)
    smem = pl.BlockSpec(memory_space=pltpu.SMEM)
    return pl.pallas_call(
        functools.partial(combine_kernel, level),
        grid=(rows // block,),
        out_shape=jax.ShapeDtypeStruct(arrived.shape, arrived.dtype),
        in_specs=[
            smem,
            smem,
            pl.BlockSpec((paths, block, columns), lambda i: (0, i, 0)),
            pl.BlockSpec((modules, block, columns), lambda i: (0, i, 0)),
        ],
        out_specs=pl.BlockSpec((paths, block, columns), lambda i: (0, i, 0)),
        scratch_shapes=[
            pltpu.VMEM((modules, block, columns), jnp.float32),
            pltpu.VMEM((modules, block, columns), arrived.dtype),
        ],
        name=f"combine_{level}",
    )(routing, factor, arrived, base)


def body(
    activations,
    cotangent,
    first_weight,
    second_weight,
    first_master,
    second_master,
    first_moment,
    second_moment,
    routing,
):
    inputs_full = lax.all_gather(activations, "mod", axis=1, tiled=True)[0]
    upstream = lax.all_gather(cotangent, "mod", axis=1, tiled=True)[0]

    def base_of(master, moment):
        return (master_factor * master + moment_factor * moment).astype(jnp.bfloat16)

    base_first = base_of(first_master, first_moment)
    base_second = base_of(second_master, second_moment)
    weight_in = first_weight[0]
    weight_out = second_weight[0]
    scale = inputs_full.shape[1] ** (-0.5)
    pre = jnp.dot(inputs_full, weight_in, preferred_element_type=jnp.float32) * scale
    hidden = jax.nn.silu(pre).astype(jnp.bfloat16)
    grad_hidden = jnp.dot(upstream, weight_out, preferred_element_type=jnp.float32) * scale
    grad_out = (
        lax.dot_general(
            upstream, hidden, (((0,), (0,)), ((), ())), preferred_element_type=jnp.float32
        )
        * scale
    )
    trained_out = (weight_out.astype(jnp.float32) - inner_rate * grad_out).astype(jnp.bfloat16)
    sigma = jax.nn.sigmoid(pre)
    grad_pre = (grad_hidden * sigma * (1.0 + pre * (1.0 - sigma))).astype(jnp.bfloat16)
    grad_in = (
        lax.dot_general(
            inputs_full, grad_pre, (((0,), (0,)), ((), ())), preferred_element_type=jnp.float32
        )
        * scale
    )
    trained_in = (weight_in.astype(jnp.float32) - inner_rate * grad_in).astype(jnp.bfloat16)

    arrived_first, arrived_second, own_first, own_second = scatter(
        trained_in, trained_out, base_first, base_second
    )
    modules = first_master.shape[0]
    taken = jnp.sum(
        (jnp.transpose(routing)[:, :, None] == jnp.arange(modules)).astype(jnp.float32), axis=1
    )
    factor = mean_factor / taken
    fresh_first = combine(0, routing, factor, arrived_first, own_first)
    fresh_second = combine(1, routing, factor, arrived_second, own_second)
    first_back, second_back = gather(fresh_first, fresh_second)
    return (first_back[None], second_back[None])


def solution(mesh):
    return jax.shard_map(
        body,
        mesh=mesh,
        in_specs=(
            P("path", "mod", None),
            P("path", "mod", None),
            P("path", None, "mod"),
            P("path", None, "mod"),
            P(None, ("path", "mod"), None),
            P(None, ("path", "mod"), None),
            P(None, ("path", "mod"), None),
            P(None, ("path", "mod"), None),
            P(),
        ),
        out_specs=(P("path", None, "mod"), P("path", None, "mod")),
        check_vma=False,
    )
```

time: 1160 us -> 626 us (0.54)
  Pallas kernels: 0 us -> 395 us
  blocking collectives: 382 us -> 0 us
  waiting for transfers between devices: 414 us -> 138 us
  local copies, waits for them, and re-layouts: 252 us -> 16.9 us
  matrix products: 77.4 us -> 40.1 us
    pallas_call x0 -> x4, Pallas kernels: none -> 395 us  [the longest x1 188 us: gather(): pl.pallas_call(functools.partial(gather_kernel, paths), out_shape=(result...]
    all_to_all x1 -> x0, blocking collectives: 382 us -> none  [to_paths(): lax.all_to_all(outgoing, ('path', 'mod'), split_axis=2, concat_axis=1, ti...]
    all_to_all x1 -> x0, waiting for transfers between devices: 280 us -> none  [to_owners(): lax.all_to_all(stacked, ('path', 'mod'), split_axis=1, concat_axis=2, til...]
    another operation x5 -> x0, local copies, waits for them, and re-layouts: 82.9 us -> none  [the longest x1 41.5 us: body(): summed = to_owners(jnp.stack((trained_in, trained_out)), onehot)]
    unnamed x10 -> x5, local copies, waits for them, and re-layouts: 59.5 us -> 16.9 us
    slice x3 -> x0, local copies, waits for them, and re-layouts: 30.1 us -> none  [the longest x2 18.2 us: body(): second_back = returned[1]]
    reshape x1 -> x0, local copies, waits for them, and re-layouts: 30 us -> none  [to_paths(): chosen.reshape(level_count, owned_rows, path_count * groups * columns)]
    dot_general x1, matrix products: 40.2 us -> 10.7 us  [body(): jnp.dot(upstream, weight_out, preferred_element_type=jnp.float32) * scale]
  transfers between devices with their start and end apart: 3 -> 2, of which waited for: 3 -> 2; matrix products, arithmetic and copies ran while one was open for 9% -> 4% of each run, Pallas kernels for 0% -> 0%
where the time goes in v1:
time: 626 us; the launch traced here: 622 us
  Pallas kernels  395 us (63%)
  waiting for transfers between devices  138 us (22%)
  matrix products  40.1 us (6%)
  other arithmetic  18.3 us (3%)
  local copies, waits for them, and re-layouts  16.9 us (3%)
  between operations  14.1 us (2%)
    pallas_call x1, Pallas kernels, gather(): pl.pallas_call(functools.partial(gather_kernel, paths), out_shape=(result...  188 us
    pallas_call x1, Pallas kernels, scatter(): pl.pallas_call(functools.partial(scatter_kernel, paths, groups), out_shap...  184 us
    all_gather x1, waiting for transfers between devices, body(): upstream = lax.all_gather(cotangent, 'mod', axis=1, tiled=True)[0]  72.7 us
    all_gather x1, waiting for transfers between devices, body(): inputs_full = lax.all_gather(activations, 'mod', axis=1, tiled=True)[0]  64 us
    pallas_call x2, Pallas kernels, combine(): pl.pallas_call(functools.partial(combine_kernel, level), grid=(rows // bl...  22.7 us
    convert_element_type x1, other arithmetic, base_of(): (master_factor * master + moment_factor * moment).astype(jnp.bfloat16)  17 us
    unnamed x5, local copies, waits for them, and re-layouts  16.9 us
  transfers between devices with their start and end apart: 2, of which 2 were waited for; matrix products, arithmetic and copies ran while one was open for 4% of the time, Pallas kernels for 0%

profile of v1, /device:TPU:1, one launch (start us, length us, event | category | flops | bytes accessed | tf_op | source)
XLA Modules:
  0.0 622.2 jit_solution(10252360335064477784)
XLA Ops:
  7.2 0.0 all-gather.5.cloned.1.call-start
  7.2 0.7 all-gather.5.cloned.1.call-update
  7.9 0.0 all-gather.3.cloned.1.call-start
  7.9 0.7 all-gather.3.cloned.1.call-update
  8.6 1.3 copy.17.routing
  10.0 0.8 convert_reduce_fusion
  10.8 0.5 broadcast_divide_fusion.factor
  11.3 17.0 %add_convert_fusion = (bf16[4,128,4096]{2,1,0:T(8,128)(2,1)}, bf16[4,128,4096]{2,1,0:T(8,128)(2,1)}) fusion(f32[4,128,4096]{2,1,0:T(8,128)} %param.16, f32[4,128,4096]{2,1,0:T(8,128)} %param.14, f32[4,128,4096]{2,1,0:T(8,128)} %param.15, f32[4,128,4096]{2,1,0:T(8,128)} %param.13), kind=kLoop, calls=%fused_computation.8 | loop fusion | flops 16777216 | bytes 41943040 | tf_op jit(solution)/shard_map/convert_element_type | solution.py:189
  28.3 64.0 %all-gather.5.cloned.1.call-done = bf16[1,512,4096]{2,1,0:T(8,128)(2,1)} async-done(((bf16[1,128,4096]{2,1,0:T(8,128)(2,1)}), bf16[1,512,4096]{2,1,0:T(8,128)(2,1)}) %all-gather.5.cloned.1.call-update) | async-done | bytes 4194320 | tf_op jit(solution)/shard_map/all_gather | solution.py:185
  92.2 8.1 %fusion.4 = f32[512,1024]{1,0:T(8,128)S(1)} fusion(bf16[1,4096,1024]{2,1,0:T(8,128)(2,1)} %param.11, bf16[1,512,4096]{2,1,0:T(8,128)(2,1)} %all-gather.5.cloned.1.call-done), kind=kOutput, calls=%fused_computation.6 | convolution fusion | flops 4294967296 | bytes 14680064 | tf_op jit(solution)/shard_map/dot_general | solution.py:196
  100.4 72.7 %all-gather.3.cloned.1.call-done = bf16[1,512,4096]{2,1,0:T(8,128)(2,1)} async-done(((bf16[1,128,4096]{2,1,0:T(8,128)(2,1)}), bf16[1,512,4096]{2,1,0:T(8,128)(2,1)}) %all-gather.3.cloned.1.call-update) | async-done | bytes 4194320 | tf_op jit(solution)/shard_map/all_gather | solution.py:186
  173.1 10.7 %multiply_convert_fusion.1 = bf16[512,1024]{1,0:T(8,128)(2,1)} fusion(f32[512,1024]{1,0:T(8,128)S(1)} %fusion.4, bf16[1,4096,1024]{2,1,0:T(8,128)(2,1)} %param.12, bf16[1,512,4096]{2,1,0:T(8,128)(2,1)} %all-gather.3.cloned.1.call-done), kind=kOutput, calls=%fused_computation.15 | convolution fusion | flops 4300734464 | bytes 15728640 | tf_op jit(solution)/shard_map/dot_general | solution.py:198
  183.8 0.0 copy-start
  183.8 11.5 %fusion.t1 = bf16[4096,1024]{1,0:T(8,128)(2,1)} fusion(bf16[1,4096,1024]{2,1,0:T(8,128)(2,1)} %param.12, bf16[1,512,4096]{2,1,0:T(8,128)(2,1)} %all-gather.3.cloned.1.call-done, f32[512,1024]{1,0:T(8,128)S(1)} %fusion.4), kind=kOutput, calls=%fused_computation.1 | convolution fusion | flops 4314890240 | bytes 23068672 | tf_op jit(solution)/shard_map/dot_general | solution.py:200
  195.2 0.0 copy-done
  195.3 9.8 %fusion.1.t0 = bf16[4096,1024]{1,0:T(8,128)(2,1)} fusion(bf16[1,4096,1024]{2,1,0:T(8,128)(2,1)} %param.11, bf16[512,1024]{1,0:T(8,128)(2,1)} %multiply_convert_fusion.1, bf16[1,512,4096]{2,1,0:T(8,128)(2,1)S(1)} %copy-done), kind=kOutput, calls=%fused_computation.3 | convolution fusion | flops 4311744512 | bytes 22020096 | tf_op jit(solution)/shard_map/dot_general | solution.py:209
  205.1 184.4 %scatter.1 = (bf16[8,512,1024]{2,1,0:T(8,128)(2,1)}, bf16[8,512,1024]{2,1,0:T(8,128)(2,1)}, bf16[4,512,1024]{2,1,0:T(8,128)(2,1)}, bf16[4,512,1024]{2,1,0:T(8,128)(2,1)}) custom-call(bf16[4096,1024]{1,0:T(8,128)(2,1)} %fusion.1.t0, bf16[4096,1024]{1,0:T(8,128)(2,1)} %fusion.t1, bf16[4,128,4096]{2,1,0:T(8,128)(2,1)} %get-tuple-element.15.b0, ...), custom_call_target="tpu_custom_call" | custom-call | tf_op jit(solution)/shard_map/scatter/pallas_call | solution.py:94
  389.4 11.3 %combine_1.1.v1 = bf16[8,512,1024]{2,1,0:T(8,128)(2,1)} custom-call(s32[8,2]{1,0:T(8,128)} %copy.17.routing, f32[2,4]{1,0:T(2,128)} %broadcast_divide_fusion.factor, bf16[8,512,1024]{2,1,0:T(8,128)(2,1)} %get-tuple-element.10.arrived, bf16[4,512,1024]{2,1,0:T(8,128)(2,1)} %get-tuple-element.11.base), custom_call_target="tpu_custom_call" | custom-call | tf_op jit(solution)/shard_map/combine_1/pallas_call | solution.py:155
  400.8 11.3 %combine_0.1.v0 = bf16[8,512,1024]{2,1,0:T(8,128)(2,1)} custom-call(s32[8,2]{1,0:T(8,128)} %copy.17.routing, f32[2,4]{1,0:T(2,128)} %broadcast_divide_fusion.factor, bf16[8,512,1024]{2,1,0:T(8,128)(2,1)} %get-tuple-element.8.arrived, bf16[4,512,1024]{2,1,0:T(8,128)(2,1)} %get-tuple-element.9.base), custom_call_target="tpu_custom_call" | custom-call | tf_op jit(solution)/shard_map/combine_0/pallas_call | solution.py:155
  412.1 187.7 %gather.1 = (bf16[4096,1024]{1,0:T(8,128)(2,1)}, bf16[4096,1024]{1,0:T(8,128)(2,1)}) custom-call(bf16[8,512,1024]{2,1,0:T(8,128)(2,1)} %combine_0.1.v0, bf16[8,512,1024]{2,1,0:T(8,128)(2,1)} %combine_1.1.v1), custom_call_target="tpu_custom_call" | custom-call | tf_op jit(solution)/shard_map/gather/pallas_call | solution.py:126
  599.8 7.8 %copy.23 = bf16[1,4096,1024]{2,1,0:T(8,128)(2,1)} copy(bf16[1,4096,1024]{2,1,0:T(8,128)(2,1)} %bitcast.35) | data formatting | bytes 16777216
  607.6 7.8 %copy.24 = bf16[1,4096,1024]{2,1,0:T(8,128)(2,1)} copy(bf16[1,4096,1024]{2,1,0:T(8,128)(2,1)} %bitcast.34) | data formatting | bytes 16777216
Async XLA Ops:
  7.2 85.1 %all-gather.5.cloned.1.call-start = ((), (), s32[]{:S(2)}) async-start(), calls=%async_computation.1 | async-start | bytes 5242880 | tf_op jit(solution)/shard_map/all_gather | solution.py:185
  7.9 165.2 %all-gather.3.cloned.1.call-start = ((), (), s32[]{:S(2)}) async-start(), calls=%async_computation | async-start | bytes 5242880 | tf_op jit(solution)/shard_map/all_gather | solution.py:186
  183.8 11.5 %copy-start = (bf16[1,512,4096]{2,1,0:T(8,128)(2,1)S(1)}, bf16[1,512,4096]{2,1,0:T(8,128)(2,1)}, u32[]{:S(2)}) copy-start(bf16[1,512,4096]{2,1,0:T(8,128)(2,1)} %all-gather.5.cloned.1.call-done) | copy-start | bytes 12582916
Sparse Core Ops, SparseCore 0:
  9.5 82.6 all-gather.4
  93.8 79.2 all-gather.2
